TPU v7x, 128 devices: a whole 4x4x4 slice. The times are simulated.
128 devices in a mesh: fit: 8 (over z, core), pair: 16 (over x, y).
Axes of the slice: x: 4, y: 4, z: 4, core: 2. Of those that a mesh axis runs over, the one named last changes fastest.
Arguments:
- metric_factor: bfloat16 [4096, 4096], P('fit'), as said below
- three_index: bfloat16 [4096, 32768], P('fit', 'pair'), may hold values from -6 to 6
- send_map: int32 [16, 16, 8], P('pair'), may hold values from 0 to 15
- pair_slots: int32 [16, 128], P('pair'), may hold values from 0 to 127, each once within a row
- pair_count: int32 [16], P('pair'), may hold values from 1 to 64, 512 in all
- orbital_energy: bfloat16 [256], P('pair'), may hold values from -2 to -0.19921875
- cabs_energy: float32 [1024], replicated, may hold values from 0.5 to 4
- coupling: bfloat16 [128, 1024], replicated, may hold values from -0.5 to 0.5
Outputs:
- projected: bfloat16 [16, 64, 128, 1024], P('pair', 'fit')
Inputs may be any that keep to these rules, and one draw needn't show every extreme that they name: `metric_factor`: diagonal entries lie between 0.6 and 1.4. `pair_slots`: each row holds every position 0 to 127 once; pair n of a row uses entries 2n and 2n + 1.
All inputs are finite; a program needn't handle non-finite values. No bound on the sum of `pair_count` on one device may be relied on, other than what follows from the above.
Results may differ from a plain program's by a relative error of at most 0.015.
Values may be sent and summed in bfloat16 or wider, within the bound.
A program may use at most 256 MiB of HBM per device.

v0:
```python
import jax
import jax.numpy as jnp
from jax import lax
from jax.sharding import PartitionSpec as P

NAUX = 4096
PAIR_BLOCK = 8


def turned_gather(arrays, axis, dims):
    turned = [jnp.moveaxis(a, dim, 0) for a, dim in zip(arrays, dims)]
    both = jnp.concatenate([t.reshape(len(t), -1) for t in turned], axis=1)
    filled, at, outs = (lax.all_gather(both, axis, axis=0, tiled=True), 0, [])
    for t, dim in zip(turned, dims):
        slab = filled[:, at : at + t[0].size].reshape(-1, *t.shape[1:])
        outs.append(jnp.moveaxis(slab, 0, dim))
        at += t[0].size
    return tuple(outs)


def on_device(
    metric_factor,
    three_index,
    send_map,
    pair_slots,
    pair_count,
    orbital_energy,
    cabs_energy,
    coupling,
):
    domain = coupling.shape[0]
    orbitals = orbital_energy.shape[0]
    local_rows = metric_factor.shape[0]
    peers = send_map.shape[1]
    capacity = send_map.shape[2]
    slot_total = pair_slots.shape[1] // 2
    fitted = jnp.dot(
        metric_factor,
        lax.all_gather(three_index, "fit", axis=0, tiled=True),
        preferred_element_type=jnp.float32,
    )
    fitted = fitted.astype(jnp.bfloat16).reshape(local_rows, orbitals, domain)
    requests = send_map.reshape(peers, capacity)
    source, energy_src = turned_gather((fitted, orbital_energy), "pair", (1, 0))
    global_ids = (jnp.arange(peers, dtype=jnp.int32)[:, None] * orbitals + requests).reshape(-1)
    pair_index = jnp.take(global_ids, pair_slots[0])
    left_index = pair_index[0::2]
    right_index = pair_index[1::2]
    live_count = pair_count[0]
    norm_scale = NAUX ** (-0.5)
    block_count = (live_count + PAIR_BLOCK - 1) // PAIR_BLOCK

    def advance(block, partial_value):
        left_ids = lax.dynamic_slice_in_dim(left_index, block * PAIR_BLOCK, PAIR_BLOCK)
        right_ids = lax.dynamic_slice_in_dim(right_index, block * PAIR_BLOCK, PAIR_BLOCK)
        left_rows = jnp.take(source, left_ids, axis=1)
        right_rows = jnp.take(source, right_ids, axis=1)
        product = jnp.einsum(
            "qsa,qsb->sab", left_rows, right_rows, preferred_element_type=jnp.float32
        )
        return lax.dynamic_update_slice_in_dim(
            partial_value, product * norm_scale, block * PAIR_BLOCK, 0
        )

    partial_value = jnp.zeros((slot_total, domain, domain), jnp.float32)
    partial_value = lax.fori_loop(0, block_count, advance, partial_value)
    share = slot_total // lax.axis_size("fit")
    first_slot = lax.axis_index("fit") * share
    exchange = lax.psum_scatter(
        partial_value.astype(jnp.bfloat16), "fit", scatter_dimension=0, tiled=True
    )
    energy_sum = jnp.take(energy_src, left_index).astype(jnp.float32) + jnp.take(
        energy_src, right_index
    ).astype(jnp.float32)
    energy_sum = lax.dynamic_slice_in_dim(energy_sum, first_slot, share, 0)
    weighted = jnp.einsum("sab,bc->sac", exchange, coupling, preferred_element_type=jnp.float32)
    denom = cabs_energy[None, None, :] - energy_sum[:, None, None]
    live_mask = first_slot + jnp.arange(share, dtype=jnp.int32) < live_count
    projected = jnp.where(live_mask[:, None, None], weighted / denom, 0.0).astype(jnp.bfloat16)
    return projected.reshape(1, share, domain, weighted.shape[2])


def solution(mesh):
    in_specs = (
        P("fit", None),
        P("fit", "pair"),
        P("pair", None, None),
        P("pair", None),
        P("pair"),
        P("pair"),
        P(),
        P(),
    )
    out_specs = P("pair", "fit", None, None)
    return jax.shard_map(
        on_device, mesh=mesh, in_specs=in_specs, out_specs=out_specs, check_vma=False
    )
```

profile of v0, /device:TPU:0, one launch (start us, length us, event | category | flops | bytes accessed | tf_op | source)
XLA Modules:
  0.0 506.7 jit_solution(18273993454955358155)
XLA Ops:
  8.1 88.6 %all-gather.3.cloned.1.call-done = bf16[4096,2048]{1,0:T(8,128)(2,1)} async-done(((bf16[512,2048]{1,0:T(8,128)(2,1)}), bf16[4096,2048]{1,0:T(8,128)(2,1)}) %all-gather.3.cloned.1.call-update) | async-done | bytes 16777232 | tf_op jit(solution)/shard_map/all_gather | solution.py:39
  96.7 13.6 %fusion.9 = bf16[64,16,8,128]{3,2,1,0:T(8,128)(2,1)S(1)} fusion(bf16[512,4096]{1,0:T(8,128)(2,1)} %param.14, bf16[4096,2048]{1,0:T(8,128)(2,1)} %all-gather.3.cloned.1.call-done), kind=kOutput, calls=%fused_computation.26 | convolution fusion | flops 8590983168 | bytes 23068672 | tf_op jit(solution)/shard_map/dot_general | solution.py:37
  110.8 1.4 copy.24
  112.2 1.5 pad_maximum_fusion
  116.4 195.1 %all-gather.5.cloned.1.call-done = bf16[256,65537]{1,0:T(8,128)(2,1)} async-done(((bf16[16,65537]{1,0:T(8,128)(2,1)}), bf16[256,65537]{1,0:T(8,128)(2,1)}) %all-gather.5.cloned.1.call-update) | async-done | bytes 33554960 | tf_op jit(solution)/shard_map/all_gather | solution.py:13
  311.5 22.9 %slice.26 = bf16[256,65536]{1,0:T(8,128)(2,1)} slice(bf16[256,65537]{1,0:T(8,128)(2,1)} %all-gather.5.cloned.1.call-done), slice={[0:256], [0:65536]} | slice | bytes 67108864 | tf_op jit(solution)/shard_map/slice | solution.py:15
  334.3 41.6 %copy.17 = bf16[256,65536]{0,1:T(8,128)(2,1)} copy(bf16[256,65536]{1,0:T(8,128)(2,1)} %slice.26) | data formatting | bytes 67108864 | tf_op jit(solution)/shard_map/slice | solution.py:15
  375.9 43.8 %copy.18 = bf16[512,256,128]{2,0,1:T(8,128)(2,1)} copy(bf16[512,256,128]{1,2,0:T(8,128)(2,1)} %bitcast.41) | data formatting | bytes 67108864 | tf_op jit(solution)/shard_map/while | solution.py:66
  419.7 1.8 broadcast_in_dim.41
  421.5 42.6 %while.10 = (s32[]{:T(128)}, bf16[64,128,128]{2,1,0:T(8,128)(2,1)}, s32[]{:T(128)}, s32[64]{0:T(128)S(1)}, bf16[512,256,128]{2,0,1:T(8,128)(2,1)}, /*index=5*/s3...) while((s32[]{:T(128)}, bf16[64,128,128]{2,1,0:T(8,128)(2,1)}, s32[]{:T(128)}, s32[64]{0:T(128)S(1)}, ...), condition=%wide.region_1.3_spmd, body=%wide.region_0.0_spmd.sunk | while | flops 135399520 | bytes 6824379 | solution.py:66
  421.6 2.0 gather_fusion.1
  423.6 2.0 gather_fusion
  426.9 2.0 gather_fusion.1
  428.9 2.0 gather_fusion
  432.2 2.0 gather_fusion.1
  434.2 2.0 gather_fusion
  436.2 1.3 fusion.21
  437.6 2.0 gather_fusion.1
  439.5 2.0 gather_fusion
  441.5 1.3 fusion.21
  442.9 2.0 gather_fusion.1
  444.9 2.0 gather_fusion
  446.8 1.3 fusion.21
  448.2 2.0 gather_fusion.1
  450.2 2.0 gather_fusion
  453.5 2.0 gather_fusion.1
  455.5 2.0 gather_fusion
  458.9 2.0 gather_fusion.1
  460.8 2.0 gather_fusion
  462.8 1.3 fusion.21
  466.8 30.3 %reduce-scatter.2.cloned.1.call-done = bf16[8,128,128]{2,1,0:T(8,128)(2,1)} async-done(((bf16[64,128,128]{2,1,0:T(8,128)(2,1)}), bf16[8,128,128]{2,1,0:T(8,128)(2,1)}) %reduce-scatter.2.cloned.1.call-update) | async-done | bytes 262160 | tf_op jit(solution)/shard_map/reduce_scatter | solution.py:69
  497.2 3.0 fusion.10
  (67 shorter events, 12.6 us)
Async XLA Ops:
  6.5 490.6 %copy-start = (bf16[128,1024]{1,0:T(8,128)(2,1)S(1)}, bf16[128,1024]{1,0:T(8,128)(2,1)}, u32[]{:S(2)}) copy-start(bf16[128,1024]{1,0:T(8,128)(2,1)} %param.21) | copy-start | bytes 786436
  6.5 90.1 %all-gather.3.cloned.1.call-start = ((), (), s32[]{:S(2)}) async-start(), calls=%async_computation.1 | async-start | bytes 18874368 | tf_op jit(solution)/shard_map/all_gather | solution.py:39
  7.3 304.2 %all-gather.5.cloned.1.call-start = ((), (), s32[]{:S(2)}) async-start(), calls=%async_computation.2 | async-start | bytes 35721216 | tf_op jit(solution)/shard_map/all_gather | solution.py:13
  112.2 2.4 copy-start.1
  112.2 2.6 copy-start.3
  113.7 383.5 %reduce-scatter.2.cloned.1.call-start = ((), (), s32[]{:S(2)}) async-start(), calls=%async_computation.3 | async-start | bytes 2359296 | tf_op jit(solution)/shard_map/reduce_scatter | solution.py:69
  421.5 45.3 %copy-start.2 = (f32[1024]{0:T(1024)S(1)}, f32[1024]{0:T(1024)}, u32[]{:S(2)}) copy-start(f32[1024]{0:T(1024)} %param.20) | copy-start | bytes 12292
Sparse Core Ops, SparseCore 0:
  9.0 87.5 all-gather.2
  113.8 197.6 all-gather.4
  464.2 32.9 reduce-scatter.1
where the time goes:
time: 509 us; the launch traced here: 507 us
  waiting for transfers between devices  315 us (62%)
  local copies, waits for them, and re-layouts  149 us (29%)
  matrix products  26.9 us (5%)
  between operations  13.9 us (3%)
    all_gather x1, waiting for transfers between devices, turned_gather(): filled, at, outs = (lax.all_gather(both, axis, axis=0, tiled=True), 0, [])  195 us
    all_gather x1, waiting for transfers between devices, on_device(): lax.all_gather(three_index, 'fit', axis=0, tiled=True)  88.6 us
    slice x3, local copies, waits for them, and re-layouts, turned_gather(): slab = filled[:, at:at + t[0].size].reshape(-1, *t.shape[1:])  65.4 us
    while x1, local copies, waits for them, and re-layouts, on_device(): partial_value = lax.fori_loop(0, block_count, advance, partial_value)  43.8 us
    reduce_scatter x1, waiting for transfers between devices, on_device(): lax.psum_scatter(partial_value.astype(jnp.bfloat16), 'fit', scatter_dimen...  30.3 us
    gather x8, local copies, waits for them, and re-layouts, advance(): left_rows = jnp.take(source, left_ids, axis=1)  15.7 us
    gather x8, local copies, waits for them, and re-layouts, advance(): right_rows = jnp.take(source, right_ids, axis=1)  15.7 us
    dot_general x1, matrix products, on_device(): jnp.dot(metric_factor, lax.all_gather(three_index, 'fit', axis=0, tiled=T...  13.6 us
  transfers between devices with their start and end apart: 3, of which 3 were waited for; matrix products, arithmetic and copies ran while one was open for 1% of the time, Pallas kernels for 0%

commit v1 on v0

--- a/solution.py
+++ b/solution.py
@@ -5,6 +5,28 @@
 
 NAUX = 4096
 PAIR_BLOCK = 8
+
+
+def laid_out(blocks, dim):
+    blocks = jnp.moveaxis(blocks, 0, dim)
+    shape = blocks.shape
+    return blocks.reshape(*shape[:dim], shape[dim] * shape[dim + 1], *shape[dim + 2 :])
+
+
+def gather_around(shard, axis, dim):
+    count = lax.axis_size(axis)
+    pairs = [(i, (i + 1) % count) for i in range(count)]
+    back = [(b, a) for a, b in pairs]
+    lower, upper = ([], [])
+    for step in range(count - 1):
+        if step % 2 == 0:
+            lower.append(lax.ppermute(lower[-1] if lower else shard, axis, pairs))
+        else:
+            upper.append(lax.ppermute(upper[-1] if upper else shard, axis, back))
+    blocks = jnp.stack([*lower[::-1], shard, *upper])
+    shift = lax.axis_index(axis) - len(lower)
+    blocks = blocks[(jnp.arange(count) - shift) % count]
+    return laid_out(blocks, dim)
 
 
 def turned_gather(arrays, axis, dims):
@@ -35,9 +57,7 @@
     capacity = send_map.shape[2]
     slot_total = pair_slots.shape[1] // 2
     fitted = jnp.dot(
-        metric_factor,
-        lax.all_gather(three_index, "fit", axis=0, tiled=True),
-        preferred_element_type=jnp.float32,
+        metric_factor, gather_around(three_index, "fit", 0), preferred_element_type=jnp.float32
     )
     fitted = fitted.astype(jnp.bfloat16).reshape(local_rows, orbitals, domain)
     requests = send_map.reshape(peers, capacity)

time: 509 us -> 570 us (1.12)
  local copies, waits for them, and re-layouts: 149 us -> 185 us
  starting transfers between devices: 0.08 us -> 9.11 us
  other arithmetic: 2.32 us -> 10.1 us
  waiting for transfers between devices: 315 us -> 322 us
    ppermute x0 -> x7, waiting for transfers between devices: none -> 98.3 us  [the longest x4 98.3 us: gather_around(): lower.append(lax.ppermute(lower[-1] if lower else shard, axis, pairs))]
    all_gather x1 -> x0, waiting for transfers between devices: 88.6 us -> none  [on_device(): lax.all_gather(three_index, 'fit', axis=0, tiled=True)]
    gather x0 -> x3, local copies, waits for them, and re-layouts: none -> 22.6 us  [gather_around(): blocks = blocks[(jnp.arange(count) - shift) % count]]
    unnamed x10 -> x23, local copies, waits for them, and re-layouts: 1.45 us -> 10.5 us
    ppermute x0 -> x7, starting transfers between devices: none -> 8.88 us  [the longest x3 8.87 us: gather_around(): upper.append(lax.ppermute(upper[-1] if upper else shard, axis, back))]
    unnamed x0 -> x1, other arithmetic: none -> 7.8 us
  transfers between devices with their start and end apart: 3 -> 9, of which waited for: 3 -> 6; matrix products, arithmetic and copies ran while one was open for 1% -> 2% of each run, Pallas kernels for 0% -> 0%
where the time goes in v1:
time: 570 us; the launch traced here: 567 us
  waiting for transfers between devices  322 us (56%)
  local copies, waits for them, and re-layouts  185 us (32%)
  matrix products  26.4 us (5%)
  between operations  14.3 us (3%)
  other arithmetic  10.1 us (2%)
  starting transfers between devices  9.11 us (2%)
    all_gather x1, waiting for transfers between devices, turned_gather(): filled, at, outs = (lax.all_gather(both, axis, axis=0, tiled=True), 0, [])  193 us
    ppermute x4, waiting for transfers between devices, gather_around(): lower.append(lax.ppermute(lower[-1] if lower else shard, axis, pairs))  98.3 us
    slice x3, local copies, waits for them, and re-layouts, turned_gather(): slab = filled[:, at:at + t[0].size].reshape(-1, *t.shape[1:])  67.6 us
    while x1, local copies, waits for them, and re-layouts, on_device(): partial_value = lax.fori_loop(0, block_count, advance, partial_value)  43.7 us
    reduce_scatter x1, waiting for transfers between devices, on_device(): lax.psum_scatter(partial_value.astype(jnp.bfloat16), 'fit', scatter_dimen...  30.3 us
    gather x3, local copies, waits for them, and re-layouts, gather_around(): blocks = blocks[(jnp.arange(count) - shift) % count]  22.6 us
    gather x8, local copies, waits for them, and re-layouts, advance(): left_rows = jnp.take(source, left_ids, axis=1)  15.7 us
    gather x8, local copies, waits for them, and re-layouts, advance(): right_rows = jnp.take(source, right_ids, axis=1)  15.7 us
  transfers between devices with their start and end apart: 9, of which 6 were waited for; matrix products, arithmetic and copies ran while one was open for 2% of the time, Pallas kernels for 0%

profile of v1, /device:TPU:0, one launch (start us, length us, event | category | flops | bytes accessed | tf_op | source)
XLA Modules:
  0.0 567.1 jit_solution(15928805245073289172)
XLA Ops:
  6.5 27.5 %collective-permute-done = bf16[512,2048]{1,0:T(8,128)(2,1)S(1)} collective-permute-done((bf16[512,2048]{1,0:T(8,128)(2,1)}, bf16[512,2048]{1,0:T(8,128)(2,1)S(1)}, u32[]{:S(2)}, u32[]{:S(2)}) %collective-permute-start) | collective-permute-done | bytes 2097184 | tf_op jit(solution)/shard_map/ppermute | solution.py:23
  34.1 3.0 collective-permute-start.4
  37.0 23.7 %collective-permute-done.1 = bf16[512,2048]{1,0:T(8,128)(2,1)S(1)} collective-permute-done((bf16[512,2048]{1,0:T(8,128)(2,1)S(1)}, bf16[512,2048]{1,0:T(8,128)(2,1)S(1)}, u32[]{:S(2)}, u32[]{:S(2)}) %collective-permute-start.1) | collective-permute-done | bytes 2097184 | tf_op jit(solution)/shard_map/ppermute | solution.py:23
  62.1 3.0 collective-permute-start.5
  65.0 23.8 %collective-permute-done.2 = bf16[512,2048]{1,0:T(8,128)(2,1)} collective-permute-done((bf16[512,2048]{1,0:T(8,128)(2,1)S(1)}, bf16[512,2048]{1,0:T(8,128)(2,1)}, u32[]{:S(2)}, u32[]{:S(2)}) %collective-permute-start.2) | collective-permute-done | bytes 2097184 | tf_op jit(solution)/shard_map/ppermute | solution.py:23
  89.6 3.0 collective-permute-start.6
  92.6 23.2 %collective-permute-done.3 = bf16[512,2048]{1,0:T(8,128)(2,1)} collective-permute-done((bf16[512,2048]{1,0:T(8,128)(2,1)}, bf16[512,2048]{1,0:T(8,128)(2,1)}, u32[]{:S(2)}, u32[]{:S(2)}) %collective-permute-start.3) | collective-permute-done | bytes 2097184 | tf_op jit(solution)/shard_map/ppermute | solution.py:23
  123.8 6.4 %fusion.14 = (bf16[8,512,1024]{2,1,0:T(8,128)(2,1)}, bf16[8,512,1024]{2,1,0:T(8,128)(2,1)}) fusion(bf16[8,512,2048]{2,1,0:T(8,128)(2,1)S(1)} %bitcast_dynamic-update-slice_fusion), kind=kLoop, calls=%fused_computation.61 | loop fusion | bytes 33554432 | tf_op jit(solution)/shard_map/gather | solution.py:28
  130.2 8.1 %gather_fusion.3 = bf16[8,512,1024]{2,1,0:T(8,128)(2,1)} fusion(bf16[8,512,1024]{2,1,0:T(8,128)(2,1)} %get-tuple-element.65, s32[1024]{0:T(1024)S(1)} %pad_clamp_fusion.4), kind=kCustom, calls=%fused_computation.5 | custom fusion | bytes 16777248 | tf_op jit(solution)/shard_map/gather | solution.py:28
  138.3 8.1 %gather_fusion.4 = bf16[8,512,1024]{2,1,0:T(8,128)(2,1)} fusion(bf16[8,512,1024]{2,1,0:T(8,128)(2,1)} %get-tuple-element.66, s32[1024]{0:T(1024)S(1)} %pad_clamp_fusion.4), kind=kCustom, calls=%fused_computation.6 | custom fusion | bytes 16777248 | tf_op jit(solution)/shard_map/gather | solution.py:28
  146.3 7.8 %pad_maximum_fusion = bf16[8,512,2048]{2,1,0:T(8,128)(2,1)S(1)} fusion(bf16[8,512,1024]{2,1,0:T(8,128)(2,1)} %gather_fusion.4, bf16[8,512,1024]{2,1,0:T(8,128)(2,1)} %gather_fusion.3), kind=kLoop, calls=%fused_computation.23 | loop fusion | flops 33554432 | bytes 33554432
  154.2 13.2 %convolution_convert_fusion = bf16[2048,512]{1,0:T(8,128)(2,1)} fusion(bf16[4096,2048]{1,0:T(8,128)(2,1)S(1)} %bitcast.59, bf16[512,4096]{1,0:T(8,128)(2,1)} %param.14), kind=kOutput, calls=%fused_computation.25 | convolution fusion | flops 8590983168 | bytes 23068672 | tf_op jit(solution)/shard_map/dot_general | solution.py:59
  167.3 3.1 copy.15
  176.1 193.4 %all-gather.2.cloned.1.call-done = bf16[256,65537]{1,0:T(8,128)(2,1)} async-done(((bf16[16,65537]{1,0:T(8,128)(2,1)}), bf16[256,65537]{1,0:T(8,128)(2,1)}) %all-gather.2.cloned.1.call-update) | async-done | bytes 33554960 | tf_op jit(solution)/shard_map/all_gather | solution.py:35
  369.4 22.8 %slice.30 = bf16[256,65536]{1,0:T(8,128)(2,1)} slice(bf16[256,65537]{1,0:T(8,128)(2,1)} %all-gather.2.cloned.1.call-done), slice={[0:256], [0:65536]} | slice | bytes 67108864 | tf_op jit(solution)/shard_map/slice | solution.py:37
  392.3 43.8 %copy.17 = bf16[256,65536]{0,1:T(8,128)(2,1)} copy(bf16[256,65536]{1,0:T(8,128)(2,1)} %slice.30) | data formatting | bytes 67108864 | tf_op jit(solution)/shard_map/slice | solution.py:37
  436.1 43.7 %copy.18 = bf16[512,256,128]{2,0,1:T(8,128)(2,1)} copy(bf16[512,256,128]{1,2,0:T(8,128)(2,1)} %bitcast.58) | data formatting | bytes 67108864 | tf_op jit(solution)/shard_map/while | solution.py:86
  481.6 42.6 %while.10 = (s32[]{:T(128)}, bf16[64,128,128]{2,1,0:T(8,128)(2,1)}, s32[]{:T(128)}, s32[64]{0:T(128)S(1)}, bf16[512,256,128]{2,0,1:T(8,128)(2,1)}, /*index=5*/s3...) while((s32[]{:T(128)}, bf16[64,128,128]{2,1,0:T(8,128)(2,1)}, s32[]{:T(128)}, s32[64]{0:T(128)S(1)}, ...), condition=%wide.region_1.3_spmd, body=%wide.region_0.2_spmd.sunk | while | flops 135399520 | bytes 6824379 | solution.py:86
  481.7 2.0 gather_fusion.1
  483.7 2.0 gather_fusion
  487.0 2.0 gather_fusion.1
  489.0 2.0 gather_fusion
  492.4 2.0 gather_fusion.1
  494.3 2.0 gather_fusion
  497.7 2.0 gather_fusion.1
  499.6 2.0 gather_fusion
  503.0 2.0 gather_fusion.1
  505.0 2.0 gather_fusion
  519.0 2.0 gather_fusion.1
  520.9 2.0 gather_fusion
  527.0 30.3 %reduce-scatter.2.cloned.1.call-done = bf16[8,128,128]{2,1,0:T(8,128)(2,1)} async-done(((bf16[64,128,128]{2,1,0:T(8,128)(2,1)}), bf16[8,128,128]{2,1,0:T(8,128)(2,1)}) %reduce-scatter.2.cloned.1.call-update) | async-done | bytes 262160 | tf_op jit(solution)/shard_map/reduce_scatter | solution.py:89
  557.3 3.0 fusion.9
  (97 shorter events, 38.3 us)
Async XLA Ops:
  6.5 550.8 %copy-start = (bf16[128,1024]{1,0:T(8,128)(2,1)S(1)}, bf16[128,1024]{1,0:T(8,128)(2,1)}, u32[]{:S(2)}) copy-start(bf16[128,1024]{1,0:T(8,128)(2,1)} %param.21) | copy-start | bytes 786436
  6.5 362.9 %all-gather.2.cloned.1.call-start = ((), (), s32[]{:S(2)}) async-start(), calls=%async_computation.1 | async-start | bytes 35721216 | tf_op jit(solution)/shard_map/all_gather | solution.py:35
  6.5 27.5 %collective-permute-start = (bf16[512,2048]{1,0:T(8,128)(2,1)}, bf16[512,2048]{1,0:T(8,128)(2,1)S(1)}, u32[]{:S(2)}, u32[]{:S(2)}) collective-permute-start(bf16[512,2048]{1,0:T(8,128)(2,1)} %param.15), channel_id=1, source_target_pairs={{0,16},{16,32},{32,48},{48,64},{64,80},{80,96},{96,112},{112,0},{1... | collective-permute-start | bytes 6291464 | tf_op jit(solution)/shard_map/ppermute | solution.py:23
  34.1 26.7 %collective-permute-start.1 = (bf16[512,2048]{1,0:T(8,128)(2,1)S(1)}, bf16[512,2048]{1,0:T(8,128)(2,1)S(1)}, u32[]{:S(2)}, u32[]{:S(2)}) collective-permute-start(bf16[512,2048]{1,0:T(8,128)(2,1)S(1)} %collective-permute-done), channel_id=1, source_target_pairs={{0,16},{16,32},{32,48},{48,64},{64,80},{80,96},{96,112},{112,0},{1... | collective-permute-start | bytes 6291464 | tf_op jit(solution)/shard_map/ppermute | solution.py:23
  34.1 28.0 %collective-permute-start.4 = (bf16[512,2048]{1,0:T(8,128)(2,1)}, bf16[512,2048]{1,0:T(8,128)(2,1)}, u32[]{:S(2)}, u32[]{:S(2)}) collective-permute-start(bf16[512,2048]{1,0:T(8,128)(2,1)} %param.15), channel_id=1, source_target_pairs={{16,0},{32,16},{48,32},{64,48},{80,64},{96,80},{112,96},{0,112},{1... | collective-permute-start | bytes 6291464 | tf_op jit(solution)/shard_map/ppermute | solution.py:25
  60.7 1.3 copy-start.2
  62.0 26.8 %collective-permute-start.2 = (bf16[512,2048]{1,0:T(8,128)(2,1)S(1)}, bf16[512,2048]{1,0:T(8,128)(2,1)}, u32[]{:S(2)}, u32[]{:S(2)}) collective-permute-start(bf16[512,2048]{1,0:T(8,128)(2,1)S(1)} %collective-permute-done.1), channel_id=1, source_target_pairs={{0,16},{16,32},{32,48},{48,64},{64,80},{80,96},{96,112},{112,0},{1... | collective-permute-start | bytes 6291464 | tf_op jit(solution)/shard_map/ppermute | solution.py:23
  62.1 27.6 %collective-permute-start.5 = (bf16[512,2048]{1,0:T(8,128)(2,1)}, bf16[512,2048]{1,0:T(8,128)(2,1)}, u32[]{:S(2)}, u32[]{:S(2)}) collective-permute-start(bf16[512,2048]{1,0:T(8,128)(2,1)} %collective-permute-done.4), channel_id=1, source_target_pairs={{16,0},{32,16},{48,32},{64,48},{80,64},{96,80},{112,96},{0,112},{1... | collective-permute-start | bytes 6291464 | tf_op jit(solution)/shard_map/ppermute | solution.py:25
  88.8 27.0 %collective-permute-start.3 = (bf16[512,2048]{1,0:T(8,128)(2,1)}, bf16[512,2048]{1,0:T(8,128)(2,1)}, u32[]{:S(2)}, u32[]{:S(2)}) collective-permute-start(bf16[512,2048]{1,0:T(8,128)(2,1)} %collective-permute-done.2), channel_id=1, source_target_pairs={{0,16},{16,32},{32,48},{48,64},{64,80},{80,96},{96,112},{112,0},{1... | collective-permute-start | bytes 6291464 | tf_op jit(solution)/shard_map/ppermute | solution.py:23
  89.6 29.9 %copy-start.3 = (bf16[512,2048]{1,0:T(8,128)(2,1)S(1)}, bf16[512,2048]{1,0:T(8,128)(2,1)}, u32[]{:S(2)}) copy-start(bf16[512,2048]{1,0:T(8,128)(2,1)} %copy-done.2) | copy-start | bytes 6291460
  89.6 30.2 %copy-start.1 = (bf16[512,2048]{1,0:T(8,128)(2,1)S(1)}, bf16[512,2048]{1,0:T(8,128)(2,1)}, u32[]{:S(2)}) copy-start(bf16[512,2048]{1,0:T(8,128)(2,1)} %param.15) | copy-start | bytes 6291460
  89.6 34.0 %collective-permute-start.6 = (bf16[512,2048]{1,0:T(8,128)(2,1)}, bf16[512,2048]{1,0:T(8,128)(2,1)S(1)}, u32[]{:S(2)}, u32[]{:S(2)}) collective-permute-start(bf16[512,2048]{1,0:T(8,128)(2,1)} %collective-permute-done.5), channel_id=1, source_target_pairs={{16,0},{32,16},{48,32},{64,48},{80,64},{96,80},{112,96},{0,112},{1... | collective-permute-start | bytes 6291464 | tf_op jit(solution)/shard_map/ppermute | solution.py:25
  167.3 6.9 %copy-start.4 = (s32[1,16,8]{1,2,0:T(8,128)S(1)}, s32[1,16,8]{1,2,0:T(8,128)}, u32[]{:S(2)}) copy-start(s32[1,16,8]{1,2,0:T(8,128)} %param.16) | copy-start | bytes 1540
  167.3 7.1 %copy-start.6 = (s32[1,128]{1,0:T(1,128)S(1)}, s32[1,128]{1,0:T(1,128)}, u32[]{:S(2)}) copy-start(s32[1,128]{1,0:T(1,128)} %param.17) | copy-start | bytes 1540
  173.2 384.1 %reduce-scatter.2.cloned.1.call-start = ((), (), s32[]{:S(2)}) async-start(), calls=%async_computation.2 | async-start | bytes 2359296 | tf_op jit(solution)/shard_map/reduce_scatter | solution.py:89
  481.6 45.3 %copy-start.5 = (f32[1024]{0:T(1024)S(1)}, f32[1024]{0:T(1024)}, u32[]{:S(2)}) copy-start(f32[1024]{0:T(1024)} %param.20) | copy-start | bytes 12292
Sparse Core Ops, SparseCore 0:
  173.3 196.0 all-gather.1
  524.3 32.9 reduce-scatter.1
